TPU v7x, 32 devices: a whole 2x2x4 slice. The times are simulated.
32 devices in a mesh: gx: 4 (over x, core), gy: 8 (over z, y).
Axes of the slice: x: 2, y: 2, z: 4, core: 2. Of those that a mesh axis runs over, the one named last changes fastest.
Arguments:
- electric: float32 [3, 64, 128, 256], P(None, 'gx', 'gy'), may hold values from -6 to 6
- magnetic: float32 [3, 64, 128, 256], P(None, 'gx', 'gy'), may hold values from -6 to 6
- aux_electric: float32 [6, 64, 128, 256], P(None, 'gx', 'gy'), may hold values from -3 to 3
- aux_magnetic: float32 [6, 64, 128, 256], P(None, 'gx', 'gy'), may hold values from -3 to 3
- grades: int32 [3, 64, 128, 256], P(None, 'gx', 'gy'), may hold values from 0 to 3
- permittivity: float32 [64, 128, 256], P('gx', 'gy'), may hold values from 1 to 8
- dipole_cell: int32 [3, 16384], P(None, ('gx', 'gy')), may hold values from 0 to 255, as said below
- dipole_port: int32 [16384], P(('gx', 'gy')), may hold values from 0 to 511
- live_count: int32 [32], P(('gx', 'gy')), may hold values from 1 to 512, as said below
- injection: bfloat16 [16384, 512], P(('gx', 'gy')), may hold values from -0.25 to 0.25
- waveform: bfloat16 [512, 16], replicated, may hold values from -6 to 6
Outputs:
- electric_out: float32 [3, 64, 128, 256], P(None, 'gx', 'gy')
- magnetic_out: float32 [3, 64, 128, 256], P(None, 'gx', 'gy')
- port_power: float32 [16, 512], replicated
Inputs may be any that keep to these rules, and one draw needn't show every extreme that they name: `dipole_cell`: slot s lies in the block of cells held by the device that holds slot s. The live slots of a device are its first live_count ones; some device has all 512 live.
All inputs are finite; a program needn't handle non-finite values.
Results may differ from a plain program's by a relative error of at most 0.0003.
Values sent between devices are 32-bit elements; how exact they have to be, the bound alone decides.
No kernel may reach another device: no remote copies, remote signals or barrier semaphores. Data moves between devices by JAX's collectives and lax.ppermute only.
A program may use at most 128 MiB of HBM per device.

v0:
```python
import jax
import jax.numpy as jnp
from jax import lax
from jax.sharding import PartitionSpec as P

courant = 0.55
absorb_keep = (0.0, 0.92, 0.75, 0.45)
absorb_take = (0.0, -0.06, -0.18, -0.35)
derivative_pairs = ((2, 1), (1, 2), (0, 2), (2, 0), (1, 0), (0, 1))


def passed_along(block, axis, distance):
    devices = range(lax.axis_size(axis))
    route = [(i - distance, i) for i in devices if i - distance in devices]
    return lax.ppermute(block, axis, route)


def difference(values, axis, plane, forward):
    length = values.shape[axis]
    if plane is None:
        shape = list(values.shape)
        shape[axis] = 1
        plane = jnp.zeros(shape, values.dtype)
    if forward:
        after = jnp.concatenate([lax.slice_in_dim(values, 1, length, axis=axis), plane], axis)
        return after - values
    before = jnp.concatenate([plane, lax.slice_in_dim(values, 0, length - 1, axis=axis)], axis)
    return values - before


def grade_table(grades, table):
    result = jnp.zeros(grades.shape, jnp.float32)
    for level in range(1, 4):
        result = result + jnp.where(grades == level, table[level], 0.0)
    return result


def curl_parts(field, auxiliary, keep, take, planes, forward):
    terms = []
    updated = []
    for number, (component, axis) in enumerate(derivative_pairs):
        plane = None
        if planes is not None and axis == 0:
            plane = planes[0][component - 1]
        if planes is not None and axis == 1:
            plane = planes[1][component // 2]
        slope = difference(field[component], axis, plane, forward)
        carried = keep[axis] * auxiliary[number] + take[axis] * slope
        terms.append(slope + carried)
        updated.append(carried)
    rotation = (terms[0] - terms[1], terms[2] - terms[3], terms[4] - terms[5])
    return (rotation, tuple(updated))


def inject(z_plane, current_now, cell_table, depth_table):
    weighted = cell_table * current_now[:, None]
    source = lax.dot_general(
        weighted, depth_table, (((0,), (0,)), ((), ())), precision=lax.Precision.HIGHEST
    )
    return z_plane - courant * source.reshape(z_plane.shape)


def read_cells(z_plane, cell_table, depth_table):
    rows = z_plane.reshape(cell_table.shape[1], depth_table.shape[1])
    picked = jnp.dot(cell_table, rows, precision=lax.Precision.HIGHEST)
    return jnp.sum(picked * depth_table, axis=1)


def note_power(record, drive, index):
    return lax.dynamic_update_slice_in_dim(record, drive[None, :], index, 0)


def local(
    electric,
    magnetic,
    aux_electric,
    aux_magnetic,
    grades,
    permittivity,
    dipole_cell,
    dipole_port,
    live_count,
    injection,
    waveform,
):
    depth_x, depth_y, depth_z = electric.shape[1:]
    slots = dipole_cell.shape[1]
    ports, steps = waveform.shape
    row_index = lax.axis_index("gx")
    col_index = lax.axis_index("gy")
    plane_cell = (dipole_cell[0] - row_index * depth_x) * depth_y + (
        dipole_cell[1] - col_index * depth_y
    )
    cell_table = (
        plane_cell[:, None] == jnp.arange(depth_x * depth_y, dtype=jnp.int32)[None, :]
    ).astype(jnp.float32)
    depth_table = (dipole_cell[2][:, None] == jnp.arange(depth_z, dtype=jnp.int32)[None, :]).astype(
        jnp.float32
    )
    live = (jnp.arange(slots, dtype=jnp.int32) < live_count[0]).astype(jnp.float32)
    current = jnp.dot(injection, waveform, preferred_element_type=jnp.float32) * live[:, None]
    members = (dipole_port[:, None] == jnp.arange(ports, dtype=jnp.int32)[None, :]).astype(
        jnp.float32
    )
    factor = courant / permittivity
    keep = grade_table(grades, absorb_keep)
    take = grade_table(grades, absorb_take)
    record = jnp.zeros((steps, slots), jnp.float32)

    def turn_parts(step, carry):
        field_e, field_h, memory_e, memory_h, record = carry
        next_x = passed_along(jnp.stack([field_e[1][0:1], field_e[2][0:1]]), "gx", -1)
        next_y = passed_along(jnp.stack([field_e[0][:, 0:1], field_e[2][:, 0:1]]), "gy", -1)
        rotation, memory_e = curl_parts(field_e, memory_e, keep, take, (next_x, next_y), True)
        field_h = tuple((field_h[number] - courant * rotation[number] for number in range(3)))
        prior_x = passed_along(jnp.stack([field_h[1][-1:], field_h[2][-1:]]), "gx", 1)
        prior_y = passed_along(jnp.stack([field_h[0][:, -1:], field_h[2][:, -1:]]), "gy", 1)
        rotation, memory_h = curl_parts(field_h, memory_h, keep, take, (prior_x, prior_y), False)
        current_now = lax.dynamic_slice_in_dim(current, step, 1, 1)[:, 0]
        z_plane = inject(field_e[2] + factor * rotation[2], current_now, cell_table, depth_table)
        field_e = (field_e[0] + factor * rotation[0], field_e[1] + factor * rotation[1], z_plane)
        drive = current_now * read_cells(z_plane, cell_table, depth_table)
        record = note_power(record, drive, step)
        return (field_e, field_h, memory_e, memory_h, record)

    start_state = (
        tuple((electric[number] for number in range(3))),
        tuple((magnetic[number] for number in range(3))),
        tuple((aux_electric[number] for number in range(6))),
        tuple((aux_magnetic[number] for number in range(6))),
        record,
    )
    parts_e, parts_h, parts_me, parts_mh, record = lax.fori_loop(0, steps, turn_parts, start_state)
    electric = jnp.stack(parts_e)
    magnetic = jnp.stack(parts_h)
    partial_value = jnp.dot(record, members, precision=lax.Precision.HIGHEST)
    port_power = lax.psum(partial_value, ("gx", "gy"))
    return (electric, magnetic, port_power)


def solution(mesh):
    in_specs = (
        P(None, "gx", "gy", None),
        P(None, "gx", "gy", None),
        P(None, "gx", "gy", None),
        P(None, "gx", "gy", None),
        P(None, "gx", "gy", None),
        P("gx", "gy", None),
        P(None, ("gx", "gy")),
        P(("gx", "gy")),
        P(("gx", "gy")),
        P(("gx", "gy"), None),
        P(),
    )
    out_specs = (P(None, "gx", "gy", None), P(None, "gx", "gy", None), P())
    return jax.shard_map(local, mesh=mesh, in_specs=in_specs, out_specs=out_specs, check_vma=False)
```

profile of v0, /device:TPU:0, one launch (start us, length us, event | category | flops | bytes accessed | tf_op | source)
XLA Modules:
  0.0 605.0 jit_solution(2541762445763992828)
XLA Ops:
  10.5 545.4 %while.50 = (s32[]{:T(128)}, f32[16,16,256]{2,1,0:T(8,128)S(1)}, f32[16,16,256]{2,1,0:T(8,128)S(1)}, f32[16,16,256]{2,1,0:T(8,128)S(1)}, f32[16,16,256]{2,1,0:T(...) while((s32[]{:T(128)}, f32[16,16,256]{2,1,0:T(8,128)S(1)}, ...), condition=%wide.region_2.3_spmd.clone, body=%wide.region_0.2_spmd.clone.sunk | while | flops 812285952 | bytes 56044672 | solution.py:133
  23.5 5.5 collective-permute-start.2
  55.6 5.4 collective-permute-start.2
  88.7 5.2 collective-permute-start.2
  95.8 5.3 collective-permute-start.3
  130.1 5.3 collective-permute-start.3
  157.3 5.2 collective-permute-start.2
  164.4 5.3 collective-permute-start.3
  191.6 5.2 collective-permute-start.2
  198.7 5.3 collective-permute-start.3
  225.9 5.2 collective-permute-start.2
  233.0 5.3 collective-permute-start.3
  260.2 5.2 collective-permute-start.2
  267.3 5.3 collective-permute-start.3
  294.5 5.2 collective-permute-start.2
  301.6 5.3 collective-permute-start.3
  335.9 5.3 collective-permute-start.3
  370.2 5.3 collective-permute-start.3
  404.5 5.3 collective-permute-start.3
  438.8 5.3 collective-permute-start.3
  473.1 5.3 collective-permute-start.3
  507.4 5.3 collective-permute-start.3
  541.7 5.3 collective-permute-start.3
  557.2 45.9 %psum.7 = f32[16,512]{1,0:T(8,128)} all-reduce(f32[16,512]{1,0:T(8,128)S(1)} %fusion.27), channel_id=1, replica_groups=mesh['gx'=4,'gy'=8] {'gx','gy'}, use_global_device_ids=true, to_apply=%region_3.4 | all-reduce | flops 8192 | bytes 65536 | tf_op jit(solution)/shard_map/psum | solution.py:137
  (1494 shorter events, 434.1 us)
Async XLA Ops:
  10.6 9.9 %collective-permute-start.1 = (f32[2,16,1,256]{3,2,1,0:T(1,128)S(1)}, f32[2,16,1,256]{3,2,1,0:T(1,128)S(1)}, u32[]{:S(2)}, u32[]{:S(2)}) collective-permute-start(f32[2,16,1,256]{3,2,1,0:T(1,128)S(1)} %pad_maximum_fusion.11), channel_id=1, source_target_pairs={{1,0},{2,1},{3,2},{4,3},{5,4},{6,5},{7,6},{9,8},{10,9},{11,10},{12... | collective-permute-start | bytes 98312 | tf_op jit(solution)/shard_map/while/body/eval_jaxpr/ppermute | solution.py:15
  23.5 10.2 %collective-permute-start.2 = (f32[2,16,1,256]{3,2,1,0:T(1,128)S(1)}, f32[2,16,1,256]{3,2,1,0:T(1,128)S(1)}, u32[]{:S(2)}, u32[]{:S(2)}) collective-permute-start(f32[2,16,1,256]{3,2,1,0:T(1,128)S(1)} %pad_maximum_fusion.12), channel_id=1, source_target_pairs={{0,1},{1,2},{2,3},{3,4},{4,5},{5,6},{6,7},{8,9},{9,10},{10,11},{11... | collective-permute-start | bytes 98312 | tf_op jit(solution)/shard_map/while/body/eval_jaxpr/ppermute | solution.py:15
  42.7 9.9 %collective-permute-start.1 = (f32[2,16,1,256]{3,2,1,0:T(1,128)S(1)}, f32[2,16,1,256]{3,2,1,0:T(1,128)S(1)}, u32[]{:S(2)}, u32[]{:S(2)}) collective-permute-start(f32[2,16,1,256]{3,2,1,0:T(1,128)S(1)} %pad_maximum_fusion.11), channel_id=1, source_target_pairs={{1,0},{2,1},{3,2},{4,3},{5,4},{6,5},{7,6},{9,8},{10,9},{11,10},{12... | collective-permute-start | bytes 98312 | tf_op jit(solution)/shard_map/while/body/eval_jaxpr/ppermute | solution.py:15
  55.6 11.2 %collective-permute-start.2 = (f32[2,16,1,256]{3,2,1,0:T(1,128)S(1)}, f32[2,16,1,256]{3,2,1,0:T(1,128)S(1)}, u32[]{:S(2)}, u32[]{:S(2)}) collective-permute-start(f32[2,16,1,256]{3,2,1,0:T(1,128)S(1)} %pad_maximum_fusion.12), channel_id=1, source_target_pairs={{0,1},{1,2},{2,3},{3,4},{4,5},{5,6},{6,7},{8,9},{9,10},{10,11},{11... | collective-permute-start | bytes 98312 | tf_op jit(solution)/shard_map/while/body/eval_jaxpr/ppermute | solution.py:15
  75.8 9.9 %collective-permute-start.1 = (f32[2,16,1,256]{3,2,1,0:T(1,128)S(1)}, f32[2,16,1,256]{3,2,1,0:T(1,128)S(1)}, u32[]{:S(2)}, u32[]{:S(2)}) collective-permute-start(f32[2,16,1,256]{3,2,1,0:T(1,128)S(1)} %pad_maximum_fusion.11), channel_id=1, source_target_pairs={{1,0},{2,1},{3,2},{4,3},{5,4},{6,5},{7,6},{9,8},{10,9},{11,10},{12... | collective-permute-start | bytes 98312 | tf_op jit(solution)/shard_map/while/body/eval_jaxpr/ppermute | solution.py:15
  88.7 12.4 %collective-permute-start.2 = (f32[2,16,1,256]{3,2,1,0:T(1,128)S(1)}, f32[2,16,1,256]{3,2,1,0:T(1,128)S(1)}, u32[]{:S(2)}, u32[]{:S(2)}) collective-permute-start(f32[2,16,1,256]{3,2,1,0:T(1,128)S(1)} %pad_maximum_fusion.12), channel_id=1, source_target_pairs={{0,1},{1,2},{2,3},{3,4},{4,5},{5,6},{6,7},{8,9},{9,10},{10,11},{11... | collective-permute-start | bytes 98312 | tf_op jit(solution)/shard_map/while/body/eval_jaxpr/ppermute | solution.py:15
  110.1 9.9 %collective-permute-start.1 = (f32[2,16,1,256]{3,2,1,0:T(1,128)S(1)}, f32[2,16,1,256]{3,2,1,0:T(1,128)S(1)}, u32[]{:S(2)}, u32[]{:S(2)}) collective-permute-start(f32[2,16,1,256]{3,2,1,0:T(1,128)S(1)} %pad_maximum_fusion.11), channel_id=1, source_target_pairs={{1,0},{2,1},{3,2},{4,3},{5,4},{6,5},{7,6},{9,8},{10,9},{11,10},{12... | collective-permute-start | bytes 98312 | tf_op jit(solution)/shard_map/while/body/eval_jaxpr/ppermute | solution.py:15
  123.0 12.4 %collective-permute-start.2 = (f32[2,16,1,256]{3,2,1,0:T(1,128)S(1)}, f32[2,16,1,256]{3,2,1,0:T(1,128)S(1)}, u32[]{:S(2)}, u32[]{:S(2)}) collective-permute-start(f32[2,16,1,256]{3,2,1,0:T(1,128)S(1)} %pad_maximum_fusion.12), channel_id=1, source_target_pairs={{0,1},{1,2},{2,3},{3,4},{4,5},{5,6},{6,7},{8,9},{9,10},{10,11},{11... | collective-permute-start | bytes 98312 | tf_op jit(solution)/shard_map/while/body/eval_jaxpr/ppermute | solution.py:15
  144.4 9.9 %collective-permute-start.1 = (f32[2,16,1,256]{3,2,1,0:T(1,128)S(1)}, f32[2,16,1,256]{3,2,1,0:T(1,128)S(1)}, u32[]{:S(2)}, u32[]{:S(2)}) collective-permute-start(f32[2,16,1,256]{3,2,1,0:T(1,128)S(1)} %pad_maximum_fusion.11), channel_id=1, source_target_pairs={{1,0},{2,1},{3,2},{4,3},{5,4},{6,5},{7,6},{9,8},{10,9},{11,10},{12... | collective-permute-start | bytes 98312 | tf_op jit(solution)/shard_map/while/body/eval_jaxpr/ppermute | solution.py:15
  157.3 12.4 %collective-permute-start.2 = (f32[2,16,1,256]{3,2,1,0:T(1,128)S(1)}, f32[2,16,1,256]{3,2,1,0:T(1,128)S(1)}, u32[]{:S(2)}, u32[]{:S(2)}) collective-permute-start(f32[2,16,1,256]{3,2,1,0:T(1,128)S(1)} %pad_maximum_fusion.12), channel_id=1, source_target_pairs={{0,1},{1,2},{2,3},{3,4},{4,5},{5,6},{6,7},{8,9},{9,10},{10,11},{11... | collective-permute-start | bytes 98312 | tf_op jit(solution)/shard_map/while/body/eval_jaxpr/ppermute | solution.py:15
  178.7 9.9 %collective-permute-start.1 = (f32[2,16,1,256]{3,2,1,0:T(1,128)S(1)}, f32[2,16,1,256]{3,2,1,0:T(1,128)S(1)}, u32[]{:S(2)}, u32[]{:S(2)}) collective-permute-start(f32[2,16,1,256]{3,2,1,0:T(1,128)S(1)} %pad_maximum_fusion.11), channel_id=1, source_target_pairs={{1,0},{2,1},{3,2},{4,3},{5,4},{6,5},{7,6},{9,8},{10,9},{11,10},{12... | collective-permute-start | bytes 98312 | tf_op jit(solution)/shard_map/while/body/eval_jaxpr/ppermute | solution.py:15
  191.6 12.4 %collective-permute-start.2 = (f32[2,16,1,256]{3,2,1,0:T(1,128)S(1)}, f32[2,16,1,256]{3,2,1,0:T(1,128)S(1)}, u32[]{:S(2)}, u32[]{:S(2)}) collective-permute-start(f32[2,16,1,256]{3,2,1,0:T(1,128)S(1)} %pad_maximum_fusion.12), channel_id=1, source_target_pairs={{0,1},{1,2},{2,3},{3,4},{4,5},{5,6},{6,7},{8,9},{9,10},{10,11},{11... | collective-permute-start | bytes 98312 | tf_op jit(solution)/shard_map/while/body/eval_jaxpr/ppermute | solution.py:15
  213.0 9.9 %collective-permute-start.1 = (f32[2,16,1,256]{3,2,1,0:T(1,128)S(1)}, f32[2,16,1,256]{3,2,1,0:T(1,128)S(1)}, u32[]{:S(2)}, u32[]{:S(2)}) collective-permute-start(f32[2,16,1,256]{3,2,1,0:T(1,128)S(1)} %pad_maximum_fusion.11), channel_id=1, source_target_pairs={{1,0},{2,1},{3,2},{4,3},{5,4},{6,5},{7,6},{9,8},{10,9},{11,10},{12... | collective-permute-start | bytes 98312 | tf_op jit(solution)/shard_map/while/body/eval_jaxpr/ppermute | solution.py:15
  225.9 12.4 %collective-permute-start.2 = (f32[2,16,1,256]{3,2,1,0:T(1,128)S(1)}, f32[2,16,1,256]{3,2,1,0:T(1,128)S(1)}, u32[]{:S(2)}, u32[]{:S(2)}) collective-permute-start(f32[2,16,1,256]{3,2,1,0:T(1,128)S(1)} %pad_maximum_fusion.12), channel_id=1, source_target_pairs={{0,1},{1,2},{2,3},{3,4},{4,5},{5,6},{6,7},{8,9},{9,10},{10,11},{11... | collective-permute-start | bytes 98312 | tf_op jit(solution)/shard_map/while/body/eval_jaxpr/ppermute | solution.py:15
  247.3 9.9 %collective-permute-start.1 = (f32[2,16,1,256]{3,2,1,0:T(1,128)S(1)}, f32[2,16,1,256]{3,2,1,0:T(1,128)S(1)}, u32[]{:S(2)}, u32[]{:S(2)}) collective-permute-start(f32[2,16,1,256]{3,2,1,0:T(1,128)S(1)} %pad_maximum_fusion.11), channel_id=1, source_target_pairs={{1,0},{2,1},{3,2},{4,3},{5,4},{6,5},{7,6},{9,8},{10,9},{11,10},{12... | collective-permute-start | bytes 98312 | tf_op jit(solution)/shard_map/while/body/eval_jaxpr/ppermute | solution.py:15
  260.2 12.4 %collective-permute-start.2 = (f32[2,16,1,256]{3,2,1,0:T(1,128)S(1)}, f32[2,16,1,256]{3,2,1,0:T(1,128)S(1)}, u32[]{:S(2)}, u32[]{:S(2)}) collective-permute-start(f32[2,16,1,256]{3,2,1,0:T(1,128)S(1)} %pad_maximum_fusion.12), channel_id=1, source_target_pairs={{0,1},{1,2},{2,3},{3,4},{4,5},{5,6},{6,7},{8,9},{9,10},{10,11},{11... | collective-permute-start | bytes 98312 | tf_op jit(solution)/shard_map/while/body/eval_jaxpr/ppermute | solution.py:15
  294.5 12.4 %collective-permute-start.2 = (f32[2,16,1,256]{3,2,1,0:T(1,128)S(1)}, f32[2,16,1,256]{3,2,1,0:T(1,128)S(1)}, u32[]{:S(2)}, u32[]{:S(2)}) collective-permute-start(f32[2,16,1,256]{3,2,1,0:T(1,128)S(1)} %pad_maximum_fusion.12), channel_id=1, source_target_pairs={{0,1},{1,2},{2,3},{3,4},{4,5},{5,6},{6,7},{8,9},{9,10},{10,11},{11... | collective-permute-start | bytes 98312 | tf_op jit(solution)/shard_map/while/body/eval_jaxpr/ppermute | solution.py:15
  328.8 12.4 %collective-permute-start.2 = (f32[2,16,1,256]{3,2,1,0:T(1,128)S(1)}, f32[2,16,1,256]{3,2,1,0:T(1,128)S(1)}, u32[]{:S(2)}, u32[]{:S(2)}) collective-permute-start(f32[2,16,1,256]{3,2,1,0:T(1,128)S(1)} %pad_maximum_fusion.12), channel_id=1, source_target_pairs={{0,1},{1,2},{2,3},{3,4},{4,5},{5,6},{6,7},{8,9},{9,10},{10,11},{11... | collective-permute-start | bytes 98312 | tf_op jit(solution)/shard_map/while/body/eval_jaxpr/ppermute | solution.py:15
  363.1 12.4 %collective-permute-start.2 = (f32[2,16,1,256]{3,2,1,0:T(1,128)S(1)}, f32[2,16,1,256]{3,2,1,0:T(1,128)S(1)}, u32[]{:S(2)}, u32[]{:S(2)}) collective-permute-start(f32[2,16,1,256]{3,2,1,0:T(1,128)S(1)} %pad_maximum_fusion.12), channel_id=1, source_target_pairs={{0,1},{1,2},{2,3},{3,4},{4,5},{5,6},{6,7},{8,9},{9,10},{10,11},{11... | collective-permute-start | bytes 98312 | tf_op jit(solution)/shard_map/while/body/eval_jaxpr/ppermute | solution.py:15
  397.4 12.4 %collective-permute-start.2 = (f32[2,16,1,256]{3,2,1,0:T(1,128)S(1)}, f32[2,16,1,256]{3,2,1,0:T(1,128)S(1)}, u32[]{:S(2)}, u32[]{:S(2)}) collective-permute-start(f32[2,16,1,256]{3,2,1,0:T(1,128)S(1)} %pad_maximum_fusion.12), channel_id=1, source_target_pairs={{0,1},{1,2},{2,3},{3,4},{4,5},{5,6},{6,7},{8,9},{9,10},{10,11},{11... | collective-permute-start | bytes 98312 | tf_op jit(solution)/shard_map/while/body/eval_jaxpr/ppermute | solution.py:15
  431.7 12.4 %collective-permute-start.2 = (f32[2,16,1,256]{3,2,1,0:T(1,128)S(1)}, f32[2,16,1,256]{3,2,1,0:T(1,128)S(1)}, u32[]{:S(2)}, u32[]{:S(2)}) collective-permute-start(f32[2,16,1,256]{3,2,1,0:T(1,128)S(1)} %pad_maximum_fusion.12), channel_id=1, source_target_pairs={{0,1},{1,2},{2,3},{3,4},{4,5},{5,6},{6,7},{8,9},{9,10},{10,11},{11... | collective-permute-start | bytes 98312 | tf_op jit(solution)/shard_map/while/body/eval_jaxpr/ppermute | solution.py:15
  466.0 12.4 %collective-permute-start.2 = (f32[2,16,1,256]{3,2,1,0:T(1,128)S(1)}, f32[2,16,1,256]{3,2,1,0:T(1,128)S(1)}, u32[]{:S(2)}, u32[]{:S(2)}) collective-permute-start(f32[2,16,1,256]{3,2,1,0:T(1,128)S(1)} %pad_maximum_fusion.12), channel_id=1, source_target_pairs={{0,1},{1,2},{2,3},{3,4},{4,5},{5,6},{6,7},{8,9},{9,10},{10,11},{11... | collective-permute-start | bytes 98312 | tf_op jit(solution)/shard_map/while/body/eval_jaxpr/ppermute | solution.py:15
  500.3 12.4 %collective-permute-start.2 = (f32[2,16,1,256]{3,2,1,0:T(1,128)S(1)}, f32[2,16,1,256]{3,2,1,0:T(1,128)S(1)}, u32[]{:S(2)}, u32[]{:S(2)}) collective-permute-start(f32[2,16,1,256]{3,2,1,0:T(1,128)S(1)} %pad_maximum_fusion.12), channel_id=1, source_target_pairs={{0,1},{1,2},{2,3},{3,4},{4,5},{5,6},{6,7},{8,9},{9,10},{10,11},{11... | collective-permute-start | bytes 98312 | tf_op jit(solution)/shard_map/while/body/eval_jaxpr/ppermute | solution.py:15
  534.6 12.4 %collective-permute-start.2 = (f32[2,16,1,256]{3,2,1,0:T(1,128)S(1)}, f32[2,16,1,256]{3,2,1,0:T(1,128)S(1)}, u32[]{:S(2)}, u32[]{:S(2)}) collective-permute-start(f32[2,16,1,256]{3,2,1,0:T(1,128)S(1)} %pad_maximum_fusion.12), channel_id=1, source_target_pairs={{0,1},{1,2},{2,3},{3,4},{4,5},{5,6},{6,7},{8,9},{9,10},{10,11},{11... | collective-permute-start | bytes 98312 | tf_op jit(solution)/shard_map/while/body/eval_jaxpr/ppermute | solution.py:15
  (464 other events, 2674.3 us)
where the time goes:
time: 612 us; the launch traced here: 605 us
  starting transfers between devices  205 us (33%)
  local copies, waits for them, and re-layouts  160 us (26%)
  other arithmetic  119 us (19%)
  matrix products  52.2 us (9%)
  blocking collectives  45.9 us (8%)
  waiting for transfers between devices  13.2 us (2%)
  loops' own time  7.44 us (1%)
    ppermute x64, starting transfers between devices, passed_along(): return lax.ppermute(block, axis, route)  205 us
    slice x96, local copies, waits for them, and re-layouts, difference(): lax.slice_in_dim(values, 1, length, axis=axis)  73.3 us
    sub x48, other arithmetic, turn_parts(): field_h[number] - courant * rotation[number]  50.2 us
    psum x1, blocking collectives, local(): port_power = lax.psum(partial_value, ('gx', 'gy'))  45.9 us
    add x16, other arithmetic, turn_parts(): field_e[1] + factor * rotation[1]  38.7 us
    while x832, local copies, waits for them, and re-layouts  36.9 us
    dot_general x16, matrix products, inject(): lax.dot_general(weighted, depth_table, (((0,), (0,)), ((), ())), precisio...  30.5 us
    dynamic_update_slice x16, local copies, waits for them, and re-layouts, note_power(): return lax.dynamic_update_slice_in_dim(record, drive[None, :], index, 0)  21.4 us
  transfers between devices with their start and end apart: 64, of which 16 were waited for; matrix products, arithmetic and copies ran while one was open for 22% of the time, Pallas kernels for 0%

commit v1 on v0

--- a/solution.py
+++ b/solution.py
@@ -7,6 +7,10 @@
 absorb_keep = (0.0, 0.92, 0.75, 0.45)
 absorb_take = (0.0, -0.06, -0.18, -0.35)
 derivative_pairs = ((2, 1), (1, 2), (0, 2), (2, 0), (1, 0), (0, 1))
+
+
+def close_loads(body):
+    return jnp.sum(lax.all_gather(body, ("gx", "gy")), axis=0)
 
 
 def passed_along(block, axis, distance):
@@ -134,7 +138,7 @@
     electric = jnp.stack(parts_e)
     magnetic = jnp.stack(parts_h)
     partial_value = jnp.dot(record, members, precision=lax.Precision.HIGHEST)
-    port_power = lax.psum(partial_value, ("gx", "gy"))
+    port_power = close_loads(partial_value)
     return (electric, magnetic, port_power)
 
 

time: 612 us -> 637 us (1.041)
  waiting for transfers between devices: 13.2 us -> 70.3 us
  blocking collectives: 45.9 us -> 0 us
  between operations: 1.44 us -> 14.9 us
    all_gather x0 -> x1, waiting for transfers between devices: none -> 57.1 us  [close_loads(): return jnp.sum(lax.all_gather(body, ('gx', 'gy')), axis=0)]
    psum x1 -> x0, blocking collectives: 45.9 us -> none  [local(): port_power = lax.psum(partial_value, ('gx', 'gy'))]
  transfers between devices with their start and end apart: 64 -> 65, of which waited for: 16 -> 17; matrix products, arithmetic and copies ran while one was open for 22% -> 21% of each run, Pallas kernels for 0% -> 0%
where the time goes in v1:
time: 637 us; the launch traced here: 630 us
  starting transfers between devices  205 us (32%)
  local copies, waits for them, and re-layouts  160 us (25%)
  other arithmetic  121 us (19%)
  waiting for transfers between devices  70.3 us (11%)
  matrix products  51.7 us (8%)
  between operations  14.9 us (2%)
  loops' own time  7.45 us (1%)
    ppermute x64, starting transfers between devices, passed_along(): return lax.ppermute(block, axis, route)  205 us
    slice x96, local copies, waits for them, and re-layouts, difference(): lax.slice_in_dim(values, 1, length, axis=axis)  73.4 us
    all_gather x1, waiting for transfers between devices, close_loads(): return jnp.sum(lax.all_gather(body, ('gx', 'gy')), axis=0)  57.1 us
    sub x48, other arithmetic, turn_parts(): field_h[number] - courant * rotation[number]  50.3 us
    add x16, other arithmetic, turn_parts(): field_e[1] + factor * rotation[1]  38.4 us
    while x832, local copies, waits for them, and re-layouts  36.6 us
    dot_general x16, matrix products, inject(): lax.dot_general(weighted, depth_table, (((0,), (0,)), ((), ())), precisio...  30.1 us
    dynamic_update_slice x16, local copies, waits for them, and re-layouts, note_power(): return lax.dynamic_update_slice_in_dim(record, drive[None, :], index, 0)  21.4 us
  transfers between devices with their start and end apart: 65, of which 17 were waited for; matrix products, arithmetic and copies ran while one was open for 21% of the time, Pallas kernels for 0%

profile of v1, /device:TPU:0, one launch (start us, length us, event | category | flops | bytes accessed | tf_op | source)
XLA Modules:
  0.0 630.5 jit_solution(7696495321807315751)
XLA Ops:
  16.2 544.6 %while.50 = (s32[]{:T(128)}, f32[16,16,256]{2,1,0:T(8,128)S(1)}, f32[16,16,256]{2,1,0:T(8,128)S(1)}, f32[16,16,256]{2,1,0:T(8,128)S(1)}, f32[16,16,256]{2,1,0:T(...) while((s32[]{:T(128)}, f32[16,16,256]{2,1,0:T(8,128)S(1)}, ...), condition=%wide.region_2.3_spmd.clone, body=%wide.region_0.2_spmd.clone.sunk | while | flops 812285952 | bytes 56044672 | solution.py:137
  29.2 5.5 collective-permute-start.2
  61.2 5.4 collective-permute-start.2
  101.3 5.3 collective-permute-start.3
  135.6 5.3 collective-permute-start.3
  169.8 5.3 collective-permute-start.3
  204.1 5.3 collective-permute-start.3
  231.3 5.2 collective-permute-start.2
  238.3 5.3 collective-permute-start.3
  265.5 5.2 collective-permute-start.2
  272.6 5.3 collective-permute-start.3
  299.8 5.2 collective-permute-start.2
  306.8 5.3 collective-permute-start.3
  334.0 5.2 collective-permute-start.2
  341.1 5.3 collective-permute-start.3
  368.3 5.2 collective-permute-start.2
  375.3 5.3 collective-permute-start.3
  402.5 5.2 collective-permute-start.2
  409.6 5.3 collective-permute-start.3
  443.8 5.3 collective-permute-start.3
  478.1 5.3 collective-permute-start.3
  512.3 5.3 collective-permute-start.3
  546.6 5.3 collective-permute-start.3
  564.6 57.1 %all-gather.3.cloned.1.call-done = f32[512,512]{1,0:T(8,128)} async-done(((f32[16,512]{1,0:T(8,128)}), f32[512,512]{1,0:T(8,128)}) %all-gather.3.cloned.1.call-update) | async-done | bytes 1048592 | tf_op jit(solution)/shard_map/all_gather | solution.py:13
  (1499 shorter events, 434.9 us)
Async XLA Ops:
  7.2 614.5 %all-gather.3.cloned.1.call-start = ((), (), s32[]{:S(2)}) async-start(), calls=%async_computation | async-start | bytes 1081344 | tf_op jit(solution)/shard_map/all_gather | solution.py:13
  16.3 9.8 %collective-permute-start.1 = (f32[2,16,1,256]{3,2,1,0:T(1,128)S(1)}, f32[2,16,1,256]{3,2,1,0:T(1,128)S(1)}, u32[]{:S(2)}, u32[]{:S(2)}) collective-permute-start(f32[2,16,1,256]{3,2,1,0:T(1,128)S(1)} %pad_maximum_fusion.11), channel_id=1, source_target_pairs={{1,0},{2,1},{3,2},{4,3},{5,4},{6,5},{7,6},{9,8},{10,9},{11,10},{12... | collective-permute-start | bytes 98312 | tf_op jit(solution)/shard_map/while/body/eval_jaxpr/ppermute | solution.py:19
  29.2 10.2 %collective-permute-start.2 = (f32[2,16,1,256]{3,2,1,0:T(1,128)S(1)}, f32[2,16,1,256]{3,2,1,0:T(1,128)S(1)}, u32[]{:S(2)}, u32[]{:S(2)}) collective-permute-start(f32[2,16,1,256]{3,2,1,0:T(1,128)S(1)} %pad_maximum_fusion.12), channel_id=1, source_target_pairs={{0,1},{1,2},{2,3},{3,4},{4,5},{5,6},{6,7},{8,9},{9,10},{10,11},{11... | collective-permute-start | bytes 98312 | tf_op jit(solution)/shard_map/while/body/eval_jaxpr/ppermute | solution.py:19
  61.2 11.2 %collective-permute-start.2 = (f32[2,16,1,256]{3,2,1,0:T(1,128)S(1)}, f32[2,16,1,256]{3,2,1,0:T(1,128)S(1)}, u32[]{:S(2)}, u32[]{:S(2)}) collective-permute-start(f32[2,16,1,256]{3,2,1,0:T(1,128)S(1)} %pad_maximum_fusion.12), channel_id=1, source_target_pairs={{0,1},{1,2},{2,3},{3,4},{4,5},{5,6},{6,7},{8,9},{9,10},{10,11},{11... | collective-permute-start | bytes 98312 | tf_op jit(solution)/shard_map/while/body/eval_jaxpr/ppermute | solution.py:19
  81.4 9.8 %collective-permute-start.1 = (f32[2,16,1,256]{3,2,1,0:T(1,128)S(1)}, f32[2,16,1,256]{3,2,1,0:T(1,128)S(1)}, u32[]{:S(2)}, u32[]{:S(2)}) collective-permute-start(f32[2,16,1,256]{3,2,1,0:T(1,128)S(1)} %pad_maximum_fusion.11), channel_id=1, source_target_pairs={{1,0},{2,1},{3,2},{4,3},{5,4},{6,5},{7,6},{9,8},{10,9},{11,10},{12... | collective-permute-start | bytes 98312 | tf_op jit(solution)/shard_map/while/body/eval_jaxpr/ppermute | solution.py:19
  94.3 12.4 %collective-permute-start.2 = (f32[2,16,1,256]{3,2,1,0:T(1,128)S(1)}, f32[2,16,1,256]{3,2,1,0:T(1,128)S(1)}, u32[]{:S(2)}, u32[]{:S(2)}) collective-permute-start(f32[2,16,1,256]{3,2,1,0:T(1,128)S(1)} %pad_maximum_fusion.12), channel_id=1, source_target_pairs={{0,1},{1,2},{2,3},{3,4},{4,5},{5,6},{6,7},{8,9},{9,10},{10,11},{11... | collective-permute-start | bytes 98312 | tf_op jit(solution)/shard_map/while/body/eval_jaxpr/ppermute | solution.py:19
  115.6 9.8 %collective-permute-start.1 = (f32[2,16,1,256]{3,2,1,0:T(1,128)S(1)}, f32[2,16,1,256]{3,2,1,0:T(1,128)S(1)}, u32[]{:S(2)}, u32[]{:S(2)}) collective-permute-start(f32[2,16,1,256]{3,2,1,0:T(1,128)S(1)} %pad_maximum_fusion.11), channel_id=1, source_target_pairs={{1,0},{2,1},{3,2},{4,3},{5,4},{6,5},{7,6},{9,8},{10,9},{11,10},{12... | collective-permute-start | bytes 98312 | tf_op jit(solution)/shard_map/while/body/eval_jaxpr/ppermute | solution.py:19
  128.5 12.4 %collective-permute-start.2 = (f32[2,16,1,256]{3,2,1,0:T(1,128)S(1)}, f32[2,16,1,256]{3,2,1,0:T(1,128)S(1)}, u32[]{:S(2)}, u32[]{:S(2)}) collective-permute-start(f32[2,16,1,256]{3,2,1,0:T(1,128)S(1)} %pad_maximum_fusion.12), channel_id=1, source_target_pairs={{0,1},{1,2},{2,3},{3,4},{4,5},{5,6},{6,7},{8,9},{9,10},{10,11},{11... | collective-permute-start | bytes 98312 | tf_op jit(solution)/shard_map/while/body/eval_jaxpr/ppermute | solution.py:19
  149.9 9.8 %collective-permute-start.1 = (f32[2,16,1,256]{3,2,1,0:T(1,128)S(1)}, f32[2,16,1,256]{3,2,1,0:T(1,128)S(1)}, u32[]{:S(2)}, u32[]{:S(2)}) collective-permute-start(f32[2,16,1,256]{3,2,1,0:T(1,128)S(1)} %pad_maximum_fusion.11), channel_id=1, source_target_pairs={{1,0},{2,1},{3,2},{4,3},{5,4},{6,5},{7,6},{9,8},{10,9},{11,10},{12... | collective-permute-start | bytes 98312 | tf_op jit(solution)/shard_map/while/body/eval_jaxpr/ppermute | solution.py:19
  162.8 12.4 %collective-permute-start.2 = (f32[2,16,1,256]{3,2,1,0:T(1,128)S(1)}, f32[2,16,1,256]{3,2,1,0:T(1,128)S(1)}, u32[]{:S(2)}, u32[]{:S(2)}) collective-permute-start(f32[2,16,1,256]{3,2,1,0:T(1,128)S(1)} %pad_maximum_fusion.12), channel_id=1, source_target_pairs={{0,1},{1,2},{2,3},{3,4},{4,5},{5,6},{6,7},{8,9},{9,10},{10,11},{11... | collective-permute-start | bytes 98312 | tf_op jit(solution)/shard_map/while/body/eval_jaxpr/ppermute | solution.py:19
  184.1 9.8 %collective-permute-start.1 = (f32[2,16,1,256]{3,2,1,0:T(1,128)S(1)}, f32[2,16,1,256]{3,2,1,0:T(1,128)S(1)}, u32[]{:S(2)}, u32[]{:S(2)}) collective-permute-start(f32[2,16,1,256]{3,2,1,0:T(1,128)S(1)} %pad_maximum_fusion.11), channel_id=1, source_target_pairs={{1,0},{2,1},{3,2},{4,3},{5,4},{6,5},{7,6},{9,8},{10,9},{11,10},{12... | collective-permute-start | bytes 98312 | tf_op jit(solution)/shard_map/while/body/eval_jaxpr/ppermute | solution.py:19
  197.0 12.4 %collective-permute-start.2 = (f32[2,16,1,256]{3,2,1,0:T(1,128)S(1)}, f32[2,16,1,256]{3,2,1,0:T(1,128)S(1)}, u32[]{:S(2)}, u32[]{:S(2)}) collective-permute-start(f32[2,16,1,256]{3,2,1,0:T(1,128)S(1)} %pad_maximum_fusion.12), channel_id=1, source_target_pairs={{0,1},{1,2},{2,3},{3,4},{4,5},{5,6},{6,7},{8,9},{9,10},{10,11},{11... | collective-permute-start | bytes 98312 | tf_op jit(solution)/shard_map/while/body/eval_jaxpr/ppermute | solution.py:19
  218.4 9.8 %collective-permute-start.1 = (f32[2,16,1,256]{3,2,1,0:T(1,128)S(1)}, f32[2,16,1,256]{3,2,1,0:T(1,128)S(1)}, u32[]{:S(2)}, u32[]{:S(2)}) collective-permute-start(f32[2,16,1,256]{3,2,1,0:T(1,128)S(1)} %pad_maximum_fusion.11), channel_id=1, source_target_pairs={{1,0},{2,1},{3,2},{4,3},{5,4},{6,5},{7,6},{9,8},{10,9},{11,10},{12... | collective-permute-start | bytes 98312 | tf_op jit(solution)/shard_map/while/body/eval_jaxpr/ppermute | solution.py:19
  231.3 12.4 %collective-permute-start.2 = (f32[2,16,1,256]{3,2,1,0:T(1,128)S(1)}, f32[2,16,1,256]{3,2,1,0:T(1,128)S(1)}, u32[]{:S(2)}, u32[]{:S(2)}) collective-permute-start(f32[2,16,1,256]{3,2,1,0:T(1,128)S(1)} %pad_maximum_fusion.12), channel_id=1, source_target_pairs={{0,1},{1,2},{2,3},{3,4},{4,5},{5,6},{6,7},{8,9},{9,10},{10,11},{11... | collective-permute-start | bytes 98312 | tf_op jit(solution)/shard_map/while/body/eval_jaxpr/ppermute | solution.py:19
  252.6 9.8 %collective-permute-start.1 = (f32[2,16,1,256]{3,2,1,0:T(1,128)S(1)}, f32[2,16,1,256]{3,2,1,0:T(1,128)S(1)}, u32[]{:S(2)}, u32[]{:S(2)}) collective-permute-start(f32[2,16,1,256]{3,2,1,0:T(1,128)S(1)} %pad_maximum_fusion.11), channel_id=1, source_target_pairs={{1,0},{2,1},{3,2},{4,3},{5,4},{6,5},{7,6},{9,8},{10,9},{11,10},{12... | collective-permute-start | bytes 98312 | tf_op jit(solution)/shard_map/while/body/eval_jaxpr/ppermute | solution.py:19
  265.5 12.4 %collective-permute-start.2 = (f32[2,16,1,256]{3,2,1,0:T(1,128)S(1)}, f32[2,16,1,256]{3,2,1,0:T(1,128)S(1)}, u32[]{:S(2)}, u32[]{:S(2)}) collective-permute-start(f32[2,16,1,256]{3,2,1,0:T(1,128)S(1)} %pad_maximum_fusion.12), channel_id=1, source_target_pairs={{0,1},{1,2},{2,3},{3,4},{4,5},{5,6},{6,7},{8,9},{9,10},{10,11},{11... | collective-permute-start | bytes 98312 | tf_op jit(solution)/shard_map/while/body/eval_jaxpr/ppermute | solution.py:19
  299.8 12.4 %collective-permute-start.2 = (f32[2,16,1,256]{3,2,1,0:T(1,128)S(1)}, f32[2,16,1,256]{3,2,1,0:T(1,128)S(1)}, u32[]{:S(2)}, u32[]{:S(2)}) collective-permute-start(f32[2,16,1,256]{3,2,1,0:T(1,128)S(1)} %pad_maximum_fusion.12), channel_id=1, source_target_pairs={{0,1},{1,2},{2,3},{3,4},{4,5},{5,6},{6,7},{8,9},{9,10},{10,11},{11... | collective-permute-start | bytes 98312 | tf_op jit(solution)/shard_map/while/body/eval_jaxpr/ppermute | solution.py:19
  334.0 12.4 %collective-permute-start.2 = (f32[2,16,1,256]{3,2,1,0:T(1,128)S(1)}, f32[2,16,1,256]{3,2,1,0:T(1,128)S(1)}, u32[]{:S(2)}, u32[]{:S(2)}) collective-permute-start(f32[2,16,1,256]{3,2,1,0:T(1,128)S(1)} %pad_maximum_fusion.12), channel_id=1, source_target_pairs={{0,1},{1,2},{2,3},{3,4},{4,5},{5,6},{6,7},{8,9},{9,10},{10,11},{11... | collective-permute-start | bytes 98312 | tf_op jit(solution)/shard_map/while/body/eval_jaxpr/ppermute | solution.py:19
  368.3 12.4 %collective-permute-start.2 = (f32[2,16,1,256]{3,2,1,0:T(1,128)S(1)}, f32[2,16,1,256]{3,2,1,0:T(1,128)S(1)}, u32[]{:S(2)}, u32[]{:S(2)}) collective-permute-start(f32[2,16,1,256]{3,2,1,0:T(1,128)S(1)} %pad_maximum_fusion.12), channel_id=1, source_target_pairs={{0,1},{1,2},{2,3},{3,4},{4,5},{5,6},{6,7},{8,9},{9,10},{10,11},{11... | collective-permute-start | bytes 98312 | tf_op jit(solution)/shard_map/while/body/eval_jaxpr/ppermute | solution.py:19
  402.5 12.4 %collective-permute-start.2 = (f32[2,16,1,256]{3,2,1,0:T(1,128)S(1)}, f32[2,16,1,256]{3,2,1,0:T(1,128)S(1)}, u32[]{:S(2)}, u32[]{:S(2)}) collective-permute-start(f32[2,16,1,256]{3,2,1,0:T(1,128)S(1)} %pad_maximum_fusion.12), channel_id=1, source_target_pairs={{0,1},{1,2},{2,3},{3,4},{4,5},{5,6},{6,7},{8,9},{9,10},{10,11},{11... | collective-permute-start | bytes 98312 | tf_op jit(solution)/shard_map/while/body/eval_jaxpr/ppermute | solution.py:19
  436.8 12.4 %collective-permute-start.2 = (f32[2,16,1,256]{3,2,1,0:T(1,128)S(1)}, f32[2,16,1,256]{3,2,1,0:T(1,128)S(1)}, u32[]{:S(2)}, u32[]{:S(2)}) collective-permute-start(f32[2,16,1,256]{3,2,1,0:T(1,128)S(1)} %pad_maximum_fusion.12), channel_id=1, source_target_pairs={{0,1},{1,2},{2,3},{3,4},{4,5},{5,6},{6,7},{8,9},{9,10},{10,11},{11... | collective-permute-start | bytes 98312 | tf_op jit(solution)/shard_map/while/body/eval_jaxpr/ppermute | solution.py:19
  471.0 12.4 %collective-permute-start.2 = (f32[2,16,1,256]{3,2,1,0:T(1,128)S(1)}, f32[2,16,1,256]{3,2,1,0:T(1,128)S(1)}, u32[]{:S(2)}, u32[]{:S(2)}) collective-permute-start(f32[2,16,1,256]{3,2,1,0:T(1,128)S(1)} %pad_maximum_fusion.12), channel_id=1, source_target_pairs={{0,1},{1,2},{2,3},{3,4},{4,5},{5,6},{6,7},{8,9},{9,10},{10,11},{11... | collective-permute-start | bytes 98312 | tf_op jit(solution)/shard_map/while/body/eval_jaxpr/ppermute | solution.py:19
  505.3 12.4 %collective-permute-start.2 = (f32[2,16,1,256]{3,2,1,0:T(1,128)S(1)}, f32[2,16,1,256]{3,2,1,0:T(1,128)S(1)}, u32[]{:S(2)}, u32[]{:S(2)}) collective-permute-start(f32[2,16,1,256]{3,2,1,0:T(1,128)S(1)} %pad_maximum_fusion.12), channel_id=1, source_target_pairs={{0,1},{1,2},{2,3},{3,4},{4,5},{5,6},{6,7},{8,9},{9,10},{10,11},{11... | collective-permute-start | bytes 98312 | tf_op jit(solution)/shard_map/while/body/eval_jaxpr/ppermute | solution.py:19
  539.5 12.4 %collective-permute-start.2 = (f32[2,16,1,256]{3,2,1,0:T(1,128)S(1)}, f32[2,16,1,256]{3,2,1,0:T(1,128)S(1)}, u32[]{:S(2)}, u32[]{:S(2)}) collective-permute-start(f32[2,16,1,256]{3,2,1,0:T(1,128)S(1)} %pad_maximum_fusion.12), channel_id=1, source_target_pairs={{0,1},{1,2},{2,3},{3,4},{4,5},{5,6},{6,7},{8,9},{9,10},{10,11},{11... | collective-permute-start | bytes 98312 | tf_op jit(solution)/shard_map/while/body/eval_jaxpr/ppermute | solution.py:19
  (466 other events, 2645.8 us)
Sparse Core Ops, SparseCore 0:
  562.9 58.8 all-gather.2
